TPU v7x, 32 devices: a whole 2x2x4 slice. The times are simulated.
32 devices in a mesh: ctx: 8 (over z, core), grp: 4 (over y, x).
Axes of the slice: x: 2, y: 2, z: 4, core: 2. Of those that a mesh axis runs over, the one named last changes fastest.
Arguments:
- queries: bfloat16 [2048, 8192], P('ctx', 'grp'), may hold values from -27 to 27, as said below
- keys: bfloat16 [2048, 1024], P('ctx'), may hold values from -27 to 27
- values: bfloat16 [2048, 1024], P('ctx'), may hold values from -6 to 6
- out_weight: bfloat16 [8192, 8192], P('grp'), may hold values from -0.0625 to 0.0625
- span_order: int32 [16], replicated, may hold values from 0 to 15, each once
- document: int32 [2048], replicated, may hold values from 0 to 3, never falling along the last dimension, each value on 1 to 1024 neighbouring positions
Outputs:
- projected: bfloat16 [2048, 8192], P('ctx', 'grp')
Inputs may be any that keep to these rules, and one draw needn't show every extreme that they name: `queries`: queries and keys are of order one, except a few rows that may be larger.
All inputs are finite; a program needn't handle non-finite values.
Results may differ from a plain program's by a relative error of at most 0.023.
Values may be sent and summed in bfloat16 or wider, within the bound.
A program may use at most 128 MiB of HBM per device.

v0:
```python
import math

import jax
import jax.numpy as jnp
from jax import lax
from jax.sharding import PartitionSpec as P

HEAD_DIM = 128
QUERY_GROUP = 8


def span_positions(span_order, first_row, count, tok_rows):
    rows = first_row + jnp.arange(count, dtype=jnp.int32)
    span_len = tok_rows // 2
    return jnp.take(span_order, rows // span_len) * span_len + rows % span_len


def attend(
    state, query_block, query_pos, query_doc, key_block, value_block, key_pos, key_doc, kv_heads
):
    out_acc, run_max, run_sum = state
    rows = query_block.shape[0]
    count = key_block.shape[0]
    group_size = query_block.shape[1] // (kv_heads * HEAD_DIM)
    grouped = query_block.reshape(rows, kv_heads, group_size, HEAD_DIM)
    key_view = key_block.reshape(count, kv_heads, HEAD_DIM)
    value_view = value_block.reshape(count, kv_heads, HEAD_DIM)
    scores = jnp.einsum("rkgd,skd->kgrs", grouped, key_view, preferred_element_type=jnp.float32)
    scores = scores * (1.0 / math.sqrt(HEAD_DIM))
    visible = (key_pos[None, :] <= query_pos[:, None]) & (key_doc[None, :] == query_doc[:, None])
    scores = jnp.where(visible, scores, -jnp.inf)
    new_max = jnp.max(scores, axis=-1)
    safe_max = jnp.where(new_max == -jnp.inf, 0.0, new_max)
    rescale = jnp.exp(run_max - safe_max)
    probs = jnp.exp(scores - safe_max[..., None])
    new_sum = run_sum * rescale + jnp.sum(probs, axis=-1)
    mixed = jnp.einsum(
        "kgrs,skd->kgrd", probs.astype(jnp.bfloat16), value_view, preferred_element_type=jnp.float32
    )
    return (out_acc * rescale[..., None] + mixed, new_max, new_sum)


def shards(queries, keys, values, out_weight, span_order, document):
    own_index = lax.axis_index("ctx")
    group_index = lax.axis_index("grp")
    tok_rows = queries.shape[0]
    local_heads = queries.shape[1] // HEAD_DIM
    kv_heads = max(1, local_heads // QUERY_GROUP)
    group_size = local_heads // kv_heads
    kv_first = group_index * local_heads // QUERY_GROUP
    key_local = lax.dynamic_slice_in_dim(keys, kv_first * HEAD_DIM, kv_heads * HEAD_DIM, 1)
    value_local = lax.dynamic_slice_in_dim(values, kv_first * HEAD_DIM, kv_heads * HEAD_DIM, 1)
    found = span_positions(span_order, own_index * tok_rows + 0, tok_rows, tok_rows)
    own_doc = jnp.take(document, found)
    start_state = (
        jnp.zeros((kv_heads, group_size, tok_rows, HEAD_DIM), jnp.float32),
        jnp.full((kv_heads, group_size, tok_rows), -jnp.inf, jnp.float32),
        jnp.zeros((kv_heads, group_size, tok_rows), jnp.float32),
    )
    pieces = (
        lax.all_gather(key_local, "ctx", axis=0, tiled=True),
        lax.all_gather(value_local, "ctx", axis=0, tiled=True),
    )
    count = pieces[0].shape[0]
    key_pos = span_positions(span_order, jnp.int32(0), count, tok_rows)
    key_doc = jnp.take(document, key_pos)
    state = attend(
        start_state, queries, found, own_doc, pieces[0], pieces[1], key_pos, key_doc, kv_heads
    )
    out_acc, run_max, run_sum = state
    attended = (out_acc / run_sum[..., None]).astype(jnp.bfloat16)
    weight_view = out_weight.reshape(kv_heads, group_size, HEAD_DIM, out_weight.shape[1])
    partial_value = jnp.einsum(
        "kgrd,kgdm->rm", attended, weight_view, preferred_element_type=jnp.float32
    )
    return lax.psum_scatter(
        partial_value.astype(jnp.bfloat16), "grp", scatter_dimension=1, tiled=True
    )


def solution(mesh):
    in_specs = (P("ctx", "grp"), P("ctx", None), P("ctx", None), P("grp", None), P(), P())
    out_specs = P("ctx", "grp")
    return jax.shard_map(shards, mesh=mesh, in_specs=in_specs, out_specs=out_specs, check_vma=False)
```

profile of v0, /device:TPU:0, one launch (start us, length us, event | category | flops | bytes accessed | tf_op | source)
XLA Modules:
  0.0 171.8 jit_solution(8921529211642206142)
XLA Ops:
  6.5 0.0 copy-start
  6.5 0.0 all-gather.3.cloned.1.call-start
  6.5 1.0 copy-done
  7.6 0.8 copy.23
  8.4 0.0 all-gather.3.cloned.1.call-update
  8.4 0.0 all-gather.5.cloned.1.call-start
  8.4 1.6 constant_dynamic-slice_fusion
  10.0 0.0 all-gather.5.cloned.1.call-update
  10.0 0.0 reduce-scatter.2.cloned.1.call-start
  10.5 1.9 %fusion.41 = (s32[1]{0:T(128)}, s32[1]{0:T(128)}, s32[1]{0:T(128)}, s32[1]{0:T(128)}, s32[1]{0:T(128)}, /*index=5*/s32[1]{0:T(128)}, s32[1]{0:T(128)}, s32[1]{0:...) fusion(s32[16]{0:T(128)} %param.10), kind=kLoop, calls=%fused_computation.107 | loop fusion | bytes 128 | tf_op jit(solution)/shard_map/jit(_take)/gather | solution.py:15
  12.4 4.3 %compare_select_fusion.3 = s32[2048,1]{0,1:T(1,128)S(1)} fusion(s32[]{:T(128)} %bitcast.9, s32[]{:T(128)} %bitcast.10, s32[]{:T(128)} %bitcast.11, s32[]{:T(128)} %bitcast.12, s32[]{:T(128)} %bitcast.13, s32[]{:T(128)} %bitcast.15, s32[]{:T(128)} %bitcast.14), kind=kLoop, calls=%fused_computation.32 | loop fusion | flops 47104 | bytes 8220 | tf_op jit(solution)/shard_map/jit(_take)/gather | solution.py:15
  16.7 4.3 %compare_select_fusion.13 = s32[256,1]{0,1:T(1,128)S(1)} fusion(s32[]{:T(128)} %bitcast.9, s32[]{:T(128)} %bitcast.10, s32[]{:T(128)} %bitcast.11, s32[]{:T(128)} %bitcast.12, s32[]{:T(128)} %bitcast.13, s32[]{:T(128)} %bitcast.15, s32[]{:T(128)} %bitcast.14, s32[]{:T(128)S(6)} %mul.68), kind=kLoop, calls=%fused_computation.78 | loop fusion | flops 7936 | bytes 1056 | tf_op jit(solution)/shard_map/jit(_take)/gather | solution.py:15
  21.2 5.5 %select_select_fusion = s32[2048]{0:T(1024)S(1)} fusion(pred[2048]{0:T(1024)(128)(4,1)S(1)} %compare_reduce_fusion, pred[2048]{0:T(1024)(128)(4,1)S(1)} %compare_reduce_fusion.1, pred[2048]{0:T(1024)(128)(4,1)S(1)} %compare_reduce_fusion.2, pred[2048]{0:T(1024)(128)(4,1)S(1)} %compare_reduce_fusion.3, pred[2048]{0:T(1024)(128)(4,1)S(1)} %compare_reduce_fusion.4, ...), kind=kLoop, calls=%fused_computation.62 | loop fusion | flops 18432 | bytes 34852 | tf_op jit(solution)/shard_map/jit(_take)/gather | solution.py:15
  26.7 10.2 %gather_fusion = s32[2048]{0:T(1024)S(1)} fusion(s32[2048]{0:T(1024)} %param.11, s32[2048]{0:T(1024)S(1)} %broadcast_clamp_fusion), kind=kCustom, calls=%fused_computation | custom fusion | bytes 24576 | tf_op jit(solution)/shard_map/jit(_take)/gather | solution.py:66
  36.9 5.5 %select_select_fusion.1 = s32[256]{0:T(256)S(1)} fusion(pred[256]{0:T(512)(128)(4,1)S(1)} %get-tuple-element.31, pred[256]{0:T(512)(128)(4,1)S(1)} %get-tuple-element.32, pred[256]{0:T(512)(128)(4,1)S(1)} %get-tuple-element.33, pred[256]{0:T(512)(128)(4,1)S(1)} %get-tuple-element.34, pred[256]{0:T(512)(128)(4,1)S(1)} %get-tuple-element.35, ...), kind=kLoop, calls=%fused_computation.102 | loop fusion | flops 2304 | bytes 4388 | tf_op jit(solution)/shard_map/jit(_take)/gather | solution.py:15
  42.4 1.9 %gather_fusion.1 = s32[256]{0:T(256)S(1)} fusion(s32[2048]{0:T(1024)} %param.11, s32[1024]{0:T(1024)S(1)} %pad_clamp_fusion), kind=kCustom, calls=%fused_computation.1 | custom fusion | bytes 3072 | tf_op jit(solution)/shard_map/jit(_take)/gather | solution.py:54
  44.4 1.5 copy.24
  45.9 1.4 compare_and_fusion
  47.3 0.0 all-gather.3.cloned.1.call-done
  47.3 14.9 %fusion.4 = (f32[2,8,256]{2,1,0:T(8,128)S(1)}, f32[2,2048,256,8]{2,1,3,0:T(8,128)}) fusion(pred[256,2048]{0,1:T(8,128)(4,1)S(1)} %compare_and_fusion, bf16[2048,2,128,1]{0,2,3,1:T(8,128)(2,1)} %bitcast.50, bf16[256,2,8,128]{3,2,1,0:T(8,128)(2,1)S(1)} %bitcast.48), kind=kOutput, calls=%fused_computation.8 | convolution fusion | flops 2172645376 | bytes 36192256 | tf_op jit(solution)/shard_map/rkgd,skd->kgrs/dot_general | solution.py:28
  62.3 20.2 %fusion.2 = (f32[2,8,256]{2,1,0:T(8,128)S(1)}, bf16[2,8,256,2048]{2,3,1,0:T(8,128)(2,1)}) fusion(f32[2,2048,256,8]{2,1,3,0:T(8,128)} %get-tuple-element.30, f32[2,8,256]{2,1,0:T(8,128)S(1)} %compare_select_fusion.2, pred[256,2048]{0,1:T(8,128)(4,1)S(1)} %compare_and_fusion), kind=kLoop, calls=%fused_computation.6 | loop fusion | flops 41938944 | bytes 50888704 | tf_op jit(solution)/shard_map/reduce_sum | solution.py:36
  82.5 0.0 all-gather.5.cloned.1.call-done
  82.6 1.3 reshape.465
  83.9 9.1 %divide_convert_fusion.clone.4 = bf16[2,8,256,128]{3,2,0,1:T(8,128)(2,1)S(1)} fusion(bf16[2,8,256,2048]{2,3,1,0:T(8,128)(2,1)} %get-tuple-element.10, bf16[2048,2,128,1]{2,1,0,3:T(2,128)(2,1)S(1)} %reshape.465, f32[2,8,256]{2,0,1:T(2,128)S(1)} %copy.15, f32[2,8,256]{2,0,1:T(2,128)S(1)} %copy.14), kind=kOutput, calls=%fused_computation.13.clone.clone.clone.1 | convolution fusion | flops 2149056512 | bytes 18907136 | tf_op jit(solution)/shard_map/kgrs,skd->kgrd/dot_general | solution.py:37
  93.0 0.0 copy-start.1
  93.0 16.8 %fusion.10 = bf16[256,8192]{1,0:T(8,128)(2,1)} fusion(bf16[2,8,128,8192]{3,2,1,0:T(8,128)(2,1)} %bitcast.57, bf16[2,8,256,128]{3,2,0,1:T(8,128)(2,1)S(1)} %divide_convert_fusion.clone.4), kind=kOutput, calls=%fused_computation.12 | convolution fusion | flops 8592031744 | bytes 38797312 | tf_op jit(solution)/shard_map/kgrd,kgdm->rm/dot_general | solution.py:73
  109.8 0.0 reduce-scatter.2.cloned.1.call-update
  109.8 55.4 %reduce-scatter.2.cloned.1.call-done = bf16[256,2048]{1,0:T(8,128)(2,1)} async-done(((bf16[256,8192]{1,0:T(8,128)(2,1)}), bf16[256,2048]{1,0:T(8,128)(2,1)}) %reduce-scatter.2.cloned.1.call-update) | async-done | bytes 1048592 | tf_op jit(solution)/shard_map/reduce_scatter | solution.py:76
  165.3 0.0 copy-done.1
  (25 shorter events, 0.7 us)
Async XLA Ops:
  6.5 1.0 copy-start
  6.5 40.8 %all-gather.3.cloned.1.call-start = ((), (), s32[]{:S(2)}) async-start(), calls=%async_computation.1 | async-start | bytes 1179648 | tf_op jit(solution)/shard_map/all_gather | solution.py:61
  8.4 74.2 %all-gather.5.cloned.1.call-start = ((), (), s32[]{:S(2)}) async-start(), calls=%async_computation.2 | async-start | bytes 1179648 | tf_op jit(solution)/shard_map/all_gather | solution.py:62
  10.0 155.3 %reduce-scatter.2.cloned.1.call-start = ((), (), s32[]{:S(2)}) async-start(), calls=%async_computation.3 | async-start | bytes 5242880 | tf_op jit(solution)/shard_map/reduce_scatter | solution.py:76
  93.0 72.3 %copy-start.1 = (bf16[256,1024]{1,0:T(8,128)(2,1)S(1)}, bf16[256,1024]{1,0:T(8,128)(2,1)}, u32[]{:S(2)}) copy-start(bf16[256,1024]{1,0:T(8,128)(2,1)} %param.7) | copy-start | bytes 1572868
Sparse Core Ops, SparseCore 0:
  8.9 26.5 all-gather.2
  37.1 21.0 all-gather.4
  110.0 55.2 reduce-scatter.1
where the time goes:
time: 173 us; the launch traced here: 172 us
  waiting for transfers between devices  55.5 us (32%)
  other arithmetic  41.8 us (24%)
  matrix products  40.8 us (24%)
  local copies, waits for them, and re-layouts  20.3 us (12%)
  between operations  13.3 us (8%)
    reduce_scatter x1, waiting for transfers between devices, shards(): lax.psum_scatter(partial_value.astype(jnp.bfloat16), 'grp', scatter_dimen...  55.4 us
    reduce_sum x1, other arithmetic, attend(): new_sum = run_sum * rescale + jnp.sum(probs, axis=-1)  20.2 us
    gather x18, other arithmetic, span_positions(): return jnp.take(span_order, rows // span_len) * span_len + rows % span_len  20 us
    dot_general x1, matrix products, shards(): jnp.einsum('kgrd,kgdm->rm', attended, weight_view, preferred_element_type...  16.8 us
    dot_general x1, matrix products, attend(): jnp.einsum('rkgd,skd->kgrs', grouped, key_view, preferred_element_type=jn...  14.9 us
    gather x1, local copies, waits for them, and re-layouts, shards(): key_doc = jnp.take(document, key_pos)  10.2 us
    dot_general x1, matrix products, attend(): jnp.einsum('kgrs,skd->kgrd', probs.astype(jnp.bfloat16), value_view, pref...  9.1 us
  transfers between devices with their start and end apart: 3, of which 1 were waited for; matrix products, arithmetic and copies ran while one was open for 43% of the time, Pallas kernels for 0%

commit v1 on v0

v1 whole, which is shorter than its diff:
```python
import functools
import math

import jax
import jax.numpy as jnp
from jax import lax
from jax.experimental import pallas as pl
from jax.experimental.pallas import tpu as pltpu
from jax.sharding import PartitionSpec as P

HEAD_DIM = 128
QUERY_GROUP = 8
CORES = 2
MESH = pl.DeviceIdType.MESH
HIDDEN = -1e30


def gather_kernel(n_ctx, first_of, k_hbm, v_hbm, k_out, v_out, local_sem, send_sem, recv_sem):
    nz = n_ctx // CORES
    me = lax.axis_index("ctx")
    group = lax.axis_index("grp")
    z, core = me // CORES, me % CORES
    partner = z * CORES + 1 - core
    width = k_out.shape[2]
    start = pl.multiple_of(first_of(group) * HEAD_DIM, HEAD_DIM)
    outs = (k_out, v_out)
    loads = [
        pltpu.make_async_copy(src.at[:, pl.ds(start, width)], dst.at[me], local_sem.at[i])
        for i, (src, dst) in enumerate(((k_hbm, k_out), (v_hbm, v_out)))
    ]
    for load in loads:
        load.start()
    barrier = pltpu.get_barrier_semaphore()
    pl.semaphore_signal(barrier, inc=1, device_id=(partner, group), device_id_type=MESH)

    @pl.when(z > 0)
    def _():
        pl.semaphore_signal(barrier, inc=1, device_id=(me - CORES, group), device_id_type=MESH)

    @pl.when(z < nz - 1)
    def _():
        pl.semaphore_signal(barrier, inc=1, device_id=(me + CORES, group), device_id_type=MESH)

    pl.semaphore_wait(barrier, 1 + jnp.minimum(z, 1) + jnp.minimum(nz - 1 - z, 1))

    def piece(way, part, chip, target):
        block = chip * CORES + core
        return pltpu.make_async_remote_copy(
            src_ref=outs[part].at[block],
            dst_ref=outs[part].at[block],
            send_sem=send_sem.at[way, part, chip],
            recv_sem=recv_sem.at[part, block],
            device_id=(target, group),
            device_id_type=MESH,
        )

    for part in range(2):
        loads[part].wait()

        @pl.when(z < nz - 1)
        def _():
            piece(0, part, z, me + CORES).start()

        @pl.when(z > 0)
        def _():
            piece(1, part, z, me - CORES).start()

        piece(2, part, z, partner).start()

    def arrived(part, chip, from_core):
        block = chip * CORES + from_core
        pltpu.make_async_copy(
            outs[part].at[block], outs[part].at[block], recv_sem.at[part, block]
        ).wait()

    for k in range(nz - 1):
        for part in range(2):

            @pl.when(z - 1 - k >= 0)
            def _():
                arrived(part, z - 1 - k, core)

                @pl.when(z < nz - 1)
                def _():
                    piece(0, part, z - 1 - k, me + CORES).start()

                piece(2, part, z - 1 - k, partner).start()

            @pl.when(z + 1 + k < nz)
            def _():
                arrived(part, z + 1 + k, core)

                @pl.when(z > 0)
                def _():
                    piece(1, part, z + 1 + k, me - CORES).start()

                piece(2, part, z + 1 + k, partner).start()

    for part in range(2):
        for chip in range(nz):
            arrived(part, chip, 1 - core)
            piece(2, part, chip, partner).wait_send()

            @pl.when((z < nz - 1) & (chip <= z))
            def _():
                piece(0, part, chip, me + CORES).wait_send()

            @pl.when((z > 0) & (chip >= z))
            def _():
                piece(1, part, chip, me - CORES).wait_send()


def gather_kv(keys, values, n_ctx, kv_heads, first_of):
    rows = keys.shape[0]
    shape = jax.ShapeDtypeStruct((n_ctx, rows, kv_heads * HEAD_DIM), keys.dtype)
    return pl.pallas_call(
        functools.partial(gather_kernel, n_ctx, first_of),
        out_shape=(shape, shape),
        in_specs=[pl.BlockSpec(memory_space=pl.ANY)] * 2,
        out_specs=(pl.BlockSpec(memory_space=pltpu.VMEM),) * 2,
        scratch_shapes=[
            pltpu.SemaphoreType.DMA((2,)),
            pltpu.SemaphoreType.DMA((3, 2, n_ctx // CORES)),
            pltpu.SemaphoreType.DMA((2, n_ctx)),
        ],
        compiler_params=pltpu.CompilerParams(collective_id=0, has_side_effects=True),
        name="gather_kv",
    )(keys, values)


def attend_kernel(
    kv_heads, order_ref, doc_ref, doc_rows, q_ref, k_hbm, v_hbm, out_ref,
    k_pos, v_ext, bias_ref, max_ref, acc_ref, sems,
):
    slots, span = k_hbm.shape[0], k_hbm.shape[1]
    heads = q_ref.shape[1] // HEAD_DIM
    group = heads // kv_heads
    me = lax.axis_index("ctx")
    copies = []
    for slot in range(slots):
        at = order_ref[slot] + 1
        copies.append(pltpu.make_async_copy(k_hbm.at[slot], k_pos.at[at], sems.at[0, slot]))
        for h in range(kv_heads):
            copies.append(
                pltpu.make_async_copy(
                    v_hbm.at[slot, :, pl.ds(h * HEAD_DIM, HEAD_DIM)],
                    v_ext.at[h, at, :, pl.ds(0, HEAD_DIM)],
                    sems.at[1 + h, slot],
                )
            )
    for copy in copies:
        copy.start()
    k_pos[0] = jnp.zeros(k_pos.shape[1:], k_pos.dtype)
    for h in range(kv_heads):
        v_ext[h, :, :, HEAD_DIM:] = jnp.ones((slots + 1, span, HEAD_DIM), v_ext.dtype)
        v_ext[h, 0, :, :HEAD_DIM] = jnp.zeros((span, HEAD_DIM), v_ext.dtype)
    for copy in copies:
        copy.wait()

    factor = math.log2(math.e) / math.sqrt(HEAD_DIM)
    row_at = lax.broadcasted_iota(jnp.int32, (span, span), 0)
    col_at = lax.broadcasted_iota(jnp.int32, (span, span), 1)

    def one_span(r, carry):
        mine = order_ref[me * 2 + r]
        rows = pl.ds(pl.multiple_of(r * span, span), span)
        first_doc = doc_ref[mine * span]
        low = jnp.int32(0)
        for t in range(slots):
            low = low + (doc_ref[t * span + span - 1] < first_doc).astype(jnp.int32)
        blocks = (mine - low) // 2 + 1
        row_doc = jnp.transpose(jnp.broadcast_to(doc_rows[mine], (span, span)))

        def block_scores(b):
            top = mine - 2 * b
            for half in range(2):
                t = top - 1 + half
                key_doc = doc_rows[jnp.maximum(t, 0)]
                key_pos = t * span + col_at
                seen = (key_doc == row_doc) & (key_pos <= mine * span + row_at) & (key_pos >= 0)
                bias_ref[:, half * span : (half + 1) * span] = jnp.where(seen, 0.0, HIDDEN)
            bias = bias_ref[...]
            pair = k_pos[pl.ds(top, 2)].reshape(2 * span, kv_heads * HEAD_DIM)
            for h in range(kv_heads):
                q = jnp.concatenate(
                    [
                        q_ref[rows, (h * group + i) * HEAD_DIM : (h * group + i + 1) * HEAD_DIM]
                        for i in range(group)
                    ],
                    axis=0,
                )
                key = pair[:, h * HEAD_DIM : (h + 1) * HEAD_DIM]
                scores = lax.dot_general(
                    q, key, (((1,), (1,)), ((), ())), preferred_element_type=jnp.float32
                )
                value = v_ext[h, pl.ds(top, 2)].reshape(2 * span, 2 * HEAD_DIM)
                yield h, scores.reshape(group, span, 2 * span) + bias[None], value

        def mix(probs, value):
            low_probs = probs.astype(jnp.bfloat16).reshape(group * span, 2 * span)
            return jnp.dot(low_probs, value, preferred_element_type=jnp.float32)

        for h, scores, value in block_scores(0):
            top = jnp.max(scores, axis=-1, keepdims=True)
            max_ref[h] = jnp.broadcast_to(top, (group, span, HEAD_DIM))
            acc_ref[h] = mix(jnp.exp2((scores - top) * factor), value)

        def more(b, carry):
            for h, scores, value in block_scores(b):
                old = max_ref[h][:, :, :1]
                top = jnp.maximum(old, jnp.max(scores, axis=-1, keepdims=True))
                max_ref[h] = jnp.broadcast_to(top, (group, span, HEAD_DIM))
                rescale = jnp.exp2((old - top) * factor).reshape(group * span, 1)
                acc_ref[h] = acc_ref[h] * rescale + mix(jnp.exp2((scores - top) * factor), value)
            return carry

        lax.fori_loop(1, blocks, more, 0)
        for h in range(kv_heads):
            mixed = acc_ref[h]
            done = (mixed[:, :HEAD_DIM] / mixed[:, HEAD_DIM:]).astype(out_ref.dtype)
            for i in range(group):
                at = (h * group + i) * HEAD_DIM
                out_ref[rows, at : at + HEAD_DIM] = done[i * span : (i + 1) * span]
        return carry

    lax.fori_loop(0, 2, one_span, 0)


def attend(queries, key_all, value_all, span_order, document, kv_heads):
    slots = span_order.shape[0]
    span = document.shape[0] // slots
    group = queries.shape[1] // HEAD_DIM // kv_heads
    width = kv_heads * HEAD_DIM
    key_all = key_all.reshape(slots, span, width)
    value_all = value_all.reshape(slots, span, width)
    smem = pl.BlockSpec(memory_space=pltpu.SMEM)
    vmem = pl.BlockSpec(memory_space=pltpu.VMEM)
    hbm = pl.BlockSpec(memory_space=pl.ANY)
    return pl.pallas_call(
        functools.partial(attend_kernel, kv_heads),
        out_shape=jax.ShapeDtypeStruct(queries.shape, queries.dtype),
        in_specs=[smem, smem, vmem, vmem, hbm, hbm],
        out_specs=vmem,
        scratch_shapes=[
            pltpu.VMEM((slots + 1, span, width), jnp.bfloat16),
            pltpu.VMEM((kv_heads, slots + 1, span, 2 * HEAD_DIM), jnp.bfloat16),
            pltpu.VMEM((span, 2 * span), jnp.float32),
            pltpu.VMEM((kv_heads, group, span, HEAD_DIM), jnp.float32),
            pltpu.VMEM((kv_heads, group * span, 2 * HEAD_DIM), jnp.float32),
            pltpu.SemaphoreType.DMA((1 + kv_heads, slots)),
        ],
        name="attend",
    )(span_order, document, document.reshape(slots, 1, span), queries, key_all, value_all)


def project_kernel(
    att_ref, w_hbm, out_ref, w_buf, send_one, got_one, send_two, got_two, own_ref,
    w_sem, sent_one, recv_one, sent_two, recv_two,
):
    me = lax.axis_index("ctx")
    group = lax.axis_index("grp")
    side = group + 1 - 2 * (group % 2)
    other = (group + 2) % 4
    far = 3 - group
    steps, _, width = w_buf.shape
    block_width = out_ref.shape[1]

    def path_sub(i):
        path = i % 2
        return path, 2 * path + (i // 2) % 2

    def block_of(i):
        path = i % 2
        first = far if i < 4 else (other if path else side)
        return first if i < 8 else ((side if path else other) if i < 12 else group)

    def fetch(i, block, sub):
        start = pl.multiple_of(block * block_width + sub * width, width)
        return pltpu.make_async_copy(w_hbm.at[:, pl.ds(start, width)], w_buf.at[i], w_sem.at[i])

    for i in range(steps):
        fetch(i, block_of(i), path_sub(i)[1]).start()

    barrier = pltpu.get_barrier_semaphore()
    for target in (side, other):
        pl.semaphore_signal(barrier, inc=1, device_id=(me, target), device_id_type=MESH)
    pl.semaphore_wait(barrier, 2)

    def product(i):
        fetch(i, group, 0).wait()
        return jnp.dot(att_ref[...], w_buf[i], preferred_element_type=jnp.float32)

    def stage_one(i):
        path = i % 2
        return pltpu.make_async_remote_copy(
            src_ref=send_one.at[i],
            dst_ref=got_one.at[i],
            send_sem=sent_one.at[i],
            recv_sem=recv_one.at[i],
            device_id=(me, (1 - path) * side + path * other),
            device_id_type=MESH,
        )

    def stage_two(j):
        path = j % 2
        return pltpu.make_async_remote_copy(
            src_ref=send_two.at[j],
            dst_ref=got_two.at[j],
            send_sem=sent_two.at[j],
            recv_sem=recv_two.at[j],
            device_id=(me, (1 - path) * other + path * side),
            device_id_type=MESH,
        )

    def first(i, carry):
        send_one[i] = product(i).astype(send_one.dtype)
        stage_one(i).start()
        return carry

    lax.fori_loop(0, 8, first, 0)

    def second(j, carry):
        part = product(8 + j)
        stage_one(j).wait_recv()
        send_two[j] = (part + got_one[j].astype(jnp.float32)).astype(send_two.dtype)
        stage_two(j).start()
        return carry

    lax.fori_loop(0, 4, second, 0)

    def third(j, carry):
        own_ref[j] = product(12 + j)
        return carry

    lax.fori_loop(0, 4, third, 0)

    for j in range(4):
        stage_one(4 + j).wait_recv()
        own_ref[j] = own_ref[j] + got_one[4 + j].astype(jnp.float32)
    for j in range(4):
        stage_two(j).wait_recv()
        at = path_sub(j)[1] * width
        out_ref[:, at : at + width] = (own_ref[j] + got_two[j].astype(jnp.float32)).astype(
            out_ref.dtype
        )
    for i in range(8):
        stage_one(i).wait_send()
    for j in range(4):
        stage_two(j).wait_send()


def project(attended, out_weight):
    rows, depth = attended.shape
    features = out_weight.shape[1]
    width = features // 16
    bf16, f32 = jnp.bfloat16, jnp.float32
    return pl.pallas_call(
        project_kernel,
        out_shape=jax.ShapeDtypeStruct((rows, features // 4), bf16),
        in_specs=[pl.BlockSpec(memory_space=pltpu.VMEM), pl.BlockSpec(memory_space=pl.ANY)],
        out_specs=pl.BlockSpec(memory_space=pltpu.VMEM),
        scratch_shapes=[
            pltpu.VMEM((16, depth, width), bf16),
            pltpu.VMEM((8, rows, width), bf16),
            pltpu.VMEM((8, rows, width), bf16),
            pltpu.VMEM((4, rows, width), bf16),
            pltpu.VMEM((4, rows, width), bf16),
            pltpu.VMEM((4, rows, width), f32),
            pltpu.SemaphoreType.DMA((16,)),
            pltpu.SemaphoreType.DMA((8,)),
            pltpu.SemaphoreType.DMA((8,)),
            pltpu.SemaphoreType.DMA((4,)),
            pltpu.SemaphoreType.DMA((4,)),
        ],
        compiler_params=pltpu.CompilerParams(
            collective_id=1, has_side_effects=True, vmem_limit_bytes=60 * 1024 * 1024
        ),
        name="project",
    )(attended, out_weight)


def shards(n_ctx, n_grp, queries, keys, values, out_weight, span_order, document):
    local_heads = queries.shape[1] // HEAD_DIM
    kv_heads = max(1, local_heads // QUERY_GROUP)
    key_all, value_all = gather_kv(
        keys, values, n_ctx, kv_heads, lambda group: group * local_heads // QUERY_GROUP
    )
    attended = attend(queries, key_all, value_all, span_order, document, kv_heads)
    if n_grp == 4:
        return project(attended, out_weight)
    partial_value = jnp.dot(attended, out_weight, preferred_element_type=jnp.float32)
    return lax.psum_scatter(
        partial_value.astype(jnp.bfloat16), "grp", scatter_dimension=1, tiled=True
    )


def solution(mesh):
    in_specs = (P("ctx", "grp"), P("ctx", None), P("ctx", None), P("grp", None), P(), P())
    body = functools.partial(shards, mesh.shape["ctx"], mesh.shape["grp"])
    return jax.shard_map(
        body, mesh=mesh, in_specs=in_specs, out_specs=P("ctx", "grp"), check_vma=False
    )
```

time: 173 us -> 83.7 us (0.48)
  the two profiles are of different devices: /device:TPU:0 before, /device:TPU:24 now
where the time goes in v1:
time: 83.7 us; the launch traced here: 84 us
  Pallas kernels  81.7 us (98%)
  local copies, waits for them, and re-layouts  2.3 us (3%)
    pallas_call x1, Pallas kernels, project(): pl.pallas_call(project_kernel, out_shape=jax.ShapeDtypeStruct((rows, feat...  38.4 us
    pallas_call x1, Pallas kernels, gather_kv(): pl.pallas_call(functools.partial(gather_kernel, n_ctx, first_of), out_sha...  22 us
    pallas_call x1, Pallas kernels, attend(): pl.pallas_call(functools.partial(attend_kernel, kv_heads), out_shape=jax....  21.3 us
    unnamed x1, local copies, waits for them, and re-layouts  2.3 us

profile of v1, /device:TPU:24, one launch (start us, length us, event | category | flops | bytes accessed | tf_op | source)
XLA Modules:
  0.0 84.0 jit_solution(14077186592360724916)
XLA Ops:
  0.0 22.0 %gather_kv.1 = (bf16[8,256,256]{2,1,0:T(8,128)(2,1)}, bf16[8,256,256]{2,1,0:T(8,128)(2,1)}) custom-call(bf16[256,1024]{1,0:T(8,128)(2,1)} %k_hbm.1, bf16[256,1024]{1,0:T(8,128)(2,1)} %v_hbm.1), custom_call_target="tpu_custom_call" | custom-call | tf_op jit(solution)/shard_map/gather_kv/pallas_call | solution.py:116
  22.0 21.3 %attend.1.att_ref = bf16[256,2048]{1,0:T(8,128)(2,1)} custom-call(s32[16]{0:T(128)} %order_ref.1, s32[2048]{0:T(1024)} %doc_ref.1, s32[16,1,128]{2,1,0:T(1,128)} %bitcast.5, bf16[256,2048]{1,0:T(8,128)(2,1)} %q_ref.1, bf16[16,128,256]{2,1,0:T(8,128)(2,1)} %bitcast.3, bf16[16,128,256]{2,1,0:T(8,128)(2,1)} %bitcast.4), custom_call_target="tpu_custom_call" | custom-call | tf_op jit(solution)/shard_map/attend/pallas_call | solution.py:239
  43.3 38.4 %project.1 = bf16[256,2048]{1,0:T(8,128)(2,1)} custom-call(bf16[256,2048]{1,0:T(8,128)(2,1)} %attend.1.att_ref, bf16[2048,8192]{1,0:T(8,128)(2,1)} %w_hbm.1), custom_call_target="tpu_custom_call" | custom-call | tf_op jit(solution)/shard_map/project/pallas_call | solution.py:357
  81.7 2.3 %copy.8 = bf16[256,2048]{1,0:T(8,128)(2,1)} copy(bf16[256,2048]{1,0:T(8,128)(2,1)} %project.1) | data formatting | bytes 2097152

commit v2 on v1

v2 whole, which is shorter than its diff:
```python
import functools
import math

import jax
import jax.numpy as jnp
from jax import lax
from jax.experimental import pallas as pl
from jax.experimental.pallas import tpu as pltpu
from jax.sharding import PartitionSpec as P

HEAD_DIM = 128
QUERY_GROUP = 8
CORES = 2
MESH = pl.DeviceIdType.MESH
HIDDEN = -1e30
UNROLL = 4


def gather_attend_kernel(
    n_ctx, kv_heads, first_of, order_ref, doc_rows, q_ref, k_hbm, v_hbm, out_ref,
    k_all, v_all, row_doc_ref, bias_ref, max_ref, acc_ref, local_sem, send_sem, recv_sem,
):
    nz = n_ctx // CORES
    me = lax.axis_index("ctx")
    group = lax.axis_index("grp")
    z, core = me // CORES, me % CORES
    partner = z * CORES + 1 - core
    tok_rows, width = k_all.shape[1], k_all.shape[2]
    span = tok_rows // 2
    heads = q_ref.shape[1] // HEAD_DIM
    shared = heads // kv_heads
    start = pl.multiple_of(first_of(group) * HEAD_DIM, HEAD_DIM)
    alls = (k_all, v_all)
    loads = [
        pltpu.make_async_copy(src.at[:, pl.ds(start, width)], dst.at[me], local_sem.at[i])
        for i, (src, dst) in enumerate(((k_hbm, k_all), (v_hbm, v_all)))
    ]
    for load in loads:
        load.start()
    barrier = pltpu.get_barrier_semaphore()
    pl.semaphore_signal(barrier, inc=1, device_id=(partner, group), device_id_type=MESH)

    @pl.when(z > 0)
    def _():
        pl.semaphore_signal(barrier, inc=1, device_id=(me - CORES, group), device_id_type=MESH)

    @pl.when(z < nz - 1)
    def _():
        pl.semaphore_signal(barrier, inc=1, device_id=(me + CORES, group), device_id_type=MESH)

    pl.semaphore_wait(barrier, 1 + jnp.minimum(z, 1) + jnp.minimum(nz - 1 - z, 1))

    def piece(way, part, chip, target):
        block = chip * CORES + core
        return pltpu.make_async_remote_copy(
            src_ref=alls[part].at[block],
            dst_ref=alls[part].at[block],
            send_sem=send_sem.at[way, part, chip],
            recv_sem=recv_sem.at[part, block],
            device_id=(target, group),
            device_id_type=MESH,
        )

    for part in range(2):
        loads[part].wait()

        @pl.when(z < nz - 1)
        def _():
            piece(0, part, z, me + CORES).start()

        @pl.when(z > 0)
        def _():
            piece(1, part, z, me - CORES).start()

        piece(2, part, z, partner).start()

    def arrived(part, chip, from_core):
        block = chip * CORES + from_core
        pltpu.make_async_copy(
            alls[part].at[block], alls[part].at[block], recv_sem.at[part, block]
        ).wait()

    max_ref[...] = jnp.full(max_ref.shape, HIDDEN, jnp.float32)
    acc_ref[...] = jnp.zeros(acc_ref.shape, jnp.float32)
    for r in range(2):
        row_doc_ref[r] = jnp.transpose(
            jnp.broadcast_to(doc_rows[order_ref[me * 2 + r]], (span, span))
        )

    factor = math.log2(math.e) / math.sqrt(HEAD_DIM)
    keys_per_step = CORES * tok_rows
    parts_of_keys = keys_per_step // HEAD_DIM
    row_at = lax.broadcasted_iota(jnp.int32, (span, span), 0)
    col_at = lax.broadcasted_iota(jnp.int32, (span, span), 1)
    near = jnp.minimum(z, nz - 1 - z)
    long_way = jnp.where(z < nz - 1 - z, 1, -1)

    def step(n, carry):
        for part in range(2):

            @pl.when((n > 0) & (z - n >= 0))
            def _():
                arrived(part, z - n, core)

                @pl.when(z < nz - 1)
                def _():
                    piece(0, part, z - n, me + CORES).start()

                piece(2, part, z - n, partner).start()

            @pl.when((n > 0) & (z + n < nz))
            def _():
                arrived(part, z + n, core)

                @pl.when(z > 0)
                def _():
                    piece(1, part, z + n, me - CORES).start()

                piece(2, part, z + n, partner).start()

        away = (n + 1) // 2
        paired = z + away * (1 - 2 * (n % 2))
        chip = jnp.where(n <= 2 * near, paired, z + long_way * (n - near))

        for slot in range(2 * CORES):
            key_span = order_ref[chip * (2 * CORES) + slot]
            key_doc = doc_rows[key_span]
            for r in range(2):
                mine = order_ref[me * 2 + r]
                seen = (key_doc == row_doc_ref[r]) & (
                    key_span * span + col_at <= mine * span + row_at
                )
                bias_ref[r * span : (r + 1) * span, slot * span : (slot + 1) * span] = jnp.where(
                    seen, 0.0, HIDDEN
                )

        for part in range(2):
            arrived(part, chip, 1 - core)

        for h in range(kv_heads):
            cols = slice(h * HEAD_DIM, (h + 1) * HEAD_DIM)

            def some_heads(at, carry):
                key = k_all[pl.ds(chip * CORES, CORES), :, cols].reshape(keys_per_step, HEAD_DIM)
                value = v_all[pl.ds(chip * CORES, CORES), :, cols].reshape(
                    keys_per_step, HEAD_DIM
                )
                value = jnp.concatenate([value, jnp.ones_like(value)], axis=1)
                picked = [h * shared + at * UNROLL + u for u in range(UNROLL)]
                scores = [
                    lax.dot_general(
                        q_ref[:, pl.ds(pl.multiple_of(head * HEAD_DIM, HEAD_DIM), HEAD_DIM)],
                        key,
                        (((1,), (1,)), ((), ())),
                        preferred_element_type=jnp.float32,
                    )
                    + bias_ref[...]
                    for head in picked
                ]
                olds = [max_ref[head] for head in picked]
                sums = [acc_ref[head] for head in picked]
                results = []
                for score, old, total in zip(scores, olds, sums):
                    top = jnp.maximum(old, jnp.max(score, axis=1, keepdims=True))
                    rescale = jnp.exp2((old - top) * factor)
                    probs = jnp.concatenate(
                        [
                            jnp.exp2(
                                (score[:, c * HEAD_DIM : (c + 1) * HEAD_DIM] - top) * factor
                            ).astype(jnp.bfloat16)
                            for c in range(parts_of_keys)
                        ],
                        axis=1,
                    )
                    mixed = jnp.dot(probs, value, preferred_element_type=jnp.float32)
                    both = jnp.concatenate([rescale, rescale], axis=1)
                    results.append((top, total * both + mixed))
                for head, (top, total) in zip(picked, results):
                    max_ref[head] = top
                    acc_ref[head] = total
                return carry

            lax.fori_loop(0, shared // UNROLL, some_heads, 0)
        return carry

    lax.fori_loop(0, nz, step, 0)

    for head in range(heads):
        total = acc_ref[head]
        out_ref[:, head * HEAD_DIM : (head + 1) * HEAD_DIM] = (
            total[:, :HEAD_DIM] / total[:, HEAD_DIM:]
        ).astype(out_ref.dtype)

    for part in range(2):
        for chip in range(nz):
            piece(2, part, chip, partner).wait_send()

            @pl.when((z < nz - 1) & (chip <= z))
            def _():
                piece(0, part, chip, me + CORES).wait_send()

            @pl.when((z > 0) & (chip >= z))
            def _():
                piece(1, part, chip, me - CORES).wait_send()


def gather_attend(queries, keys, values, span_order, document, n_ctx, kv_heads, first_of):
    slots = span_order.shape[0]
    span = document.shape[0] // slots
    rows = queries.shape[0]
    heads = queries.shape[1] // HEAD_DIM
    smem = pl.BlockSpec(memory_space=pltpu.SMEM)
    vmem = pl.BlockSpec(memory_space=pltpu.VMEM)
    hbm = pl.BlockSpec(memory_space=pl.ANY)
    f32, bf16 = jnp.float32, jnp.bfloat16
    return pl.pallas_call(
        functools.partial(gather_attend_kernel, n_ctx, kv_heads, first_of),
        out_shape=jax.ShapeDtypeStruct(queries.shape, queries.dtype),
        in_specs=[smem, vmem, vmem, hbm, hbm],
        out_specs=vmem,
        scratch_shapes=[
            pltpu.VMEM((n_ctx, rows, kv_heads * HEAD_DIM), bf16),
            pltpu.VMEM((n_ctx, rows, kv_heads * HEAD_DIM), bf16),
            pltpu.VMEM((2, span, span), jnp.int32),
            pltpu.VMEM((rows, CORES * rows), f32),
            pltpu.VMEM((heads, rows, HEAD_DIM), f32),
            pltpu.VMEM((heads, rows, 2 * HEAD_DIM), f32),
            pltpu.SemaphoreType.DMA((2,)),
            pltpu.SemaphoreType.DMA((3, 2, n_ctx // CORES)),
            pltpu.SemaphoreType.DMA((2, n_ctx)),
        ],
        compiler_params=pltpu.CompilerParams(collective_id=0, has_side_effects=True),
        name="gather_attend",
    )(span_order, document.reshape(slots, 1, span), queries, keys, values)


def project_kernel(
    att_ref, w_hbm, out_ref, w_buf, send_one, got_one, send_two, got_two, own_ref,
    w_sem, sent_one, recv_one, sent_two, recv_two,
):
    me = lax.axis_index("ctx")
    group = lax.axis_index("grp")
    side = group + 1 - 2 * (group % 2)
    other = (group + 2) % 4
    far = 3 - group
    steps, _, width = w_buf.shape
    block_width = out_ref.shape[1]

    def path_sub(i):
        path = i % 2
        return path, 2 * path + (i // 2) % 2

    def block_of(i):
        path = i % 2
        first = far if i < 4 else (other if path else side)
        return first if i < 8 else ((side if path else other) if i < 12 else group)

    def fetch(i, block, sub):
        start = pl.multiple_of(block * block_width + sub * width, width)
        return pltpu.make_async_copy(w_hbm.at[:, pl.ds(start, width)], w_buf.at[i], w_sem.at[i])

    for i in range(steps):
        fetch(i, block_of(i), path_sub(i)[1]).start()

    barrier = pltpu.get_barrier_semaphore()
    for target in (side, other):
        pl.semaphore_signal(barrier, inc=1, device_id=(me, target), device_id_type=MESH)
    pl.semaphore_wait(barrier, 2)

    def product(i):
        fetch(i, group, 0).wait()
        return jnp.dot(att_ref[...], w_buf[i], preferred_element_type=jnp.float32)

    def stage_one(i):
        path = i % 2
        return pltpu.make_async_remote_copy(
            src_ref=send_one.at[i],
            dst_ref=got_one.at[i],
            send_sem=sent_one.at[i],
            recv_sem=recv_one.at[i],
            device_id=(me, (1 - path) * side + path * other),
            device_id_type=MESH,
        )

    def stage_two(j):
        path = j % 2
        return pltpu.make_async_remote_copy(
            src_ref=send_two.at[j],
            dst_ref=got_two.at[j],
            send_sem=sent_two.at[j],
            recv_sem=recv_two.at[j],
            device_id=(me, (1 - path) * other + path * side),
            device_id_type=MESH,
        )

    def first(i, carry):
        send_one[i] = product(i).astype(send_one.dtype)
        stage_one(i).start()
        return carry

    lax.fori_loop(0, 8, first, 0)

    def second(j, carry):
        part = product(8 + j)
        stage_one(j).wait_recv()
        send_two[j] = (part + got_one[j].astype(jnp.float32)).astype(send_two.dtype)
        stage_two(j).start()
        return carry

    lax.fori_loop(0, 4, second, 0)

    def third(j, carry):
        own_ref[j] = product(12 + j)
        return carry

    lax.fori_loop(0, 4, third, 0)

    for j in range(4):
        stage_one(4 + j).wait_recv()
        own_ref[j] = own_ref[j] + got_one[4 + j].astype(jnp.float32)
    for j in range(4):
        stage_two(j).wait_recv()
        at = path_sub(j)[1] * width
        out_ref[:, at : at + width] = (own_ref[j] + got_two[j].astype(jnp.float32)).astype(
            out_ref.dtype
        )
    for i in range(8):
        stage_one(i).wait_send()
    for j in range(4):
        stage_two(j).wait_send()


def project(attended, out_weight):
    rows, depth = attended.shape
    features = out_weight.shape[1]
    width = features // 16
    bf16, f32 = jnp.bfloat16, jnp.float32
    return pl.pallas_call(
        project_kernel,
        out_shape=jax.ShapeDtypeStruct((rows, features // 4), bf16),
        in_specs=[pl.BlockSpec(memory_space=pltpu.VMEM), pl.BlockSpec(memory_space=pl.ANY)],
        out_specs=pl.BlockSpec(memory_space=pltpu.VMEM),
        scratch_shapes=[
            pltpu.VMEM((16, depth, width), bf16),
            pltpu.VMEM((8, rows, width), bf16),
            pltpu.VMEM((8, rows, width), bf16),
            pltpu.VMEM((4, rows, width), bf16),
            pltpu.VMEM((4, rows, width), bf16),
            pltpu.VMEM((4, rows, width), f32),
            pltpu.SemaphoreType.DMA((16,)),
            pltpu.SemaphoreType.DMA((8,)),
            pltpu.SemaphoreType.DMA((8,)),
            pltpu.SemaphoreType.DMA((4,)),
            pltpu.SemaphoreType.DMA((4,)),
        ],
        compiler_params=pltpu.CompilerParams(
            collective_id=1, has_side_effects=True, vmem_limit_bytes=60 * 1024 * 1024
        ),
        name="project",
    )(attended, out_weight)


def shards(n_ctx, n_grp, queries, keys, values, out_weight, span_order, document):
    local_heads = queries.shape[1] // HEAD_DIM
    kv_heads = max(1, local_heads // QUERY_GROUP)
    attended = gather_attend(
        queries, keys, values, span_order, document, n_ctx, kv_heads,
        lambda group: group * local_heads // QUERY_GROUP,
    )
    if n_grp == 4:
        return project(attended, out_weight)
    partial_value = jnp.dot(attended, out_weight, preferred_element_type=jnp.float32)
    return lax.psum_scatter(
        partial_value.astype(jnp.bfloat16), "grp", scatter_dimension=1, tiled=True
    )


def solution(mesh):
    in_specs = (P("ctx", "grp"), P("ctx", None), P("ctx", None), P("grp", None), P(), P())
    body = functools.partial(shards, mesh.shape["ctx"], mesh.shape["grp"])
    return jax.shard_map(
        body, mesh=mesh, in_specs=in_specs, out_specs=P("ctx", "grp"), check_vma=False
    )
```

time: 83.7 us -> 74.7 us (0.89)
  the two profiles are of different devices: /device:TPU:24 before, /device:TPU:0 now
where the time goes in v2:
time: 74.7 us; the launch traced here: 74.5 us
  Pallas kernels  72.1 us (97%)
  local copies, waits for them, and re-layouts  2.3 us (3%)
    pallas_call x1, Pallas kernels, project(): pl.pallas_call(project_kernel, out_shape=jax.ShapeDtypeStruct((rows, feat...  42.2 us
    pallas_call x1, Pallas kernels, gather_attend(): pl.pallas_call(functools.partial(gather_attend_kernel, n_ctx, kv_heads, f...  29.9 us
    unnamed x1, local copies, waits for them, and re-layouts  2.3 us

profile of v2, /device:TPU:0, one launch (start us, length us, event | category | flops | bytes accessed | tf_op | source)
XLA Modules:
  0.0 74.5 jit_solution(3128795720409736301)
XLA Ops:
  0.0 29.9 %gather_attend.1.att_ref = bf16[256,2048]{1,0:T(8,128)(2,1)} custom-call(s32[16]{0:T(128)} %order_ref.1, s32[16,1,128]{2,1,0:T(1,128)} %bitcast.1, bf16[256,2048]{1,0:T(8,128)(2,1)} %q_ref.1, bf16[256,1024]{1,0:T(8,128)(2,1)} %k_hbm.1, bf16[256,1024]{1,0:T(8,128)(2,1)} %v_hbm.1), custom_call_target="tpu_custom_call" | custom-call | tf_op jit(solution)/shard_map/gather_attend/pallas_call | solution.py:216
  29.9 42.2 %project.1 = bf16[256,2048]{1,0:T(8,128)(2,1)} custom-call(bf16[256,2048]{1,0:T(8,128)(2,1)} %gather_attend.1.att_ref, bf16[2048,8192]{1,0:T(8,128)(2,1)} %w_hbm.1), custom_call_target="tpu_custom_call" | custom-call | tf_op jit(solution)/shard_map/project/pallas_call | solution.py:338
  72.1 2.3 %copy.8 = bf16[256,2048]{1,0:T(8,128)(2,1)} copy(bf16[256,2048]{1,0:T(8,128)(2,1)} %project.1) | data formatting | bytes 2097152

commit v3 on v2

--- a/solution.py
+++ b/solution.py
@@ -14,6 +14,7 @@
 MESH = pl.DeviceIdType.MESH
 HIDDEN = -1e30
 UNROLL = 4
+AHEAD = 3
 
 
 def gather_attend_kernel(
@@ -252,14 +253,16 @@
 
     def block_of(i):
         path = i % 2
-        first = far if i < 4 else (other if path else side)
-        return first if i < 8 else ((side if path else other) if i < 12 else group)
+        crossed = jnp.where(path == 1, side, other)
+        straight = jnp.where(path == 1, other, side)
+        first = jnp.where(i < 4, far, straight)
+        return jnp.where(i < 8, first, jnp.where(i < 12, crossed, group))
 
     def fetch(i, block, sub):
         start = pl.multiple_of(block * block_width + sub * width, width)
         return pltpu.make_async_copy(w_hbm.at[:, pl.ds(start, width)], w_buf.at[i], w_sem.at[i])
 
-    for i in range(steps):
+    for i in range(AHEAD):
         fetch(i, block_of(i), path_sub(i)[1]).start()
 
     barrier = pltpu.get_barrier_semaphore()
@@ -269,6 +272,11 @@
 
     def product(i):
         fetch(i, group, 0).wait()
+
+        @pl.when(i + AHEAD < steps)
+        def _():
+            fetch(i + AHEAD, block_of(i + AHEAD), path_sub(i + AHEAD)[1]).start()
+
         return jnp.dot(att_ref[...], w_buf[i], preferred_element_type=jnp.float32)
 
     def stage_one(i):

time: 74.7 us -> 74.7 us (level)
  no operation moved by 1% of the time
where the time goes in v3:
time: 74.7 us; the launch traced here: 74.5 us
  Pallas kernels  72.1 us (97%)
  local copies, waits for them, and re-layouts  2.3 us (3%)
    pallas_call x1, Pallas kernels, project(): pl.pallas_call(project_kernel, out_shape=jax.ShapeDtypeStruct((rows, feat...  42.3 us
    pallas_call x1, Pallas kernels, gather_attend(): pl.pallas_call(functools.partial(gather_attend_kernel, n_ctx, kv_heads, f...  29.9 us
    unnamed x1, local copies, waits for them, and re-layouts  2.3 us

profile of v3, /device:TPU:0, one launch (start us, length us, event | category | flops | bytes accessed | tf_op | source)
XLA Modules:
  0.0 74.5 jit_solution(12486117278755511613)
XLA Ops:
  0.0 29.9 %gather_attend.1.att_ref = bf16[256,2048]{1,0:T(8,128)(2,1)} custom-call(s32[16]{0:T(128)} %order_ref.1, s32[16,1,128]{2,1,0:T(1,128)} %bitcast.1, bf16[256,2048]{1,0:T(8,128)(2,1)} %q_ref.1, bf16[256,1024]{1,0:T(8,128)(2,1)} %k_hbm.1, bf16[256,1024]{1,0:T(8,128)(2,1)} %v_hbm.1), custom_call_target="tpu_custom_call" | custom-call | tf_op jit(solution)/shard_map/gather_attend/pallas_call | solution.py:217
  29.9 42.3 %project.1 = bf16[256,2048]{1,0:T(8,128)(2,1)} custom-call(bf16[256,2048]{1,0:T(8,128)(2,1)} %gather_attend.1.att_ref, bf16[2048,8192]{1,0:T(8,128)(2,1)} %w_hbm.1), custom_call_target="tpu_custom_call" | custom-call | tf_op jit(solution)/shard_map/project/pallas_call | solution.py:346
  72.2 2.3 %copy.8 = bf16[256,2048]{1,0:T(8,128)(2,1)} copy(bf16[256,2048]{1,0:T(8,128)(2,1)} %project.1) | data formatting | bytes 2097152
